TPU v7x, 32 devices: a whole 2x2x4 slice. The times are simulated.
32 devices in a mesh: grp: 1, blk: 8 (over z, y), node: 4 (over x, core), pair: 1.
Axes of the slice: x: 2, y: 2, z: 4, core: 2. Of those that a mesh axis runs over, the one named last changes fastest.
Arguments:
- query: bfloat16 [4608, 1280], P(('grp', 'blk', 'node'), 'pair'), may hold values from -600 to 600
- key: bfloat16 [4608, 1280], P(('grp', 'blk', 'node'), 'pair'), may hold values from -25 to 25
- value: bfloat16 [4608, 1280], P(('grp', 'blk', 'node'), 'pair'), may hold values from -6 to 6
- out_weight: bfloat16 [1280, 1280], P('pair'), may hold values from -0.15625 to 0.15625
Outputs:
- mixed: bfloat16 [4608, 1280], P(('grp', 'blk', 'node', 'pair'))
All inputs are finite; a program needn't handle non-finite values.
Results may differ from a plain program's by a relative error of at most 0.011.
Values may be sent and summed in bfloat16 or wider, within the bound.
A program may use at most 128 MiB of HBM per device.

v0:
```python
import math
import jax
import jax.numpy as jnp
from jax import lax
from jax.sharding import PartitionSpec as P

HD = 64
lowest = -1e30


def block_rows(count):
    size = count
    while size > 1024 and size % 2 == 0:
        size = size // 2
    return size


def attend(carry, keys_piece, values_piece, queries):
    count = keys_piece.shape[0]
    size = block_rows(count)
    q_rows, heads, width = queries.shape
    scale = 1.0 / math.sqrt(width)

    def update(turn, state):
        peak, total, accum = state
        key_block = lax.dynamic_slice_in_dim(keys_piece, turn * size, size, 0).reshape(
            size, heads, width
        )
        value_block = lax.dynamic_slice_in_dim(values_piece, turn * size, size, 0).reshape(
            size, heads, width
        )
        scores = (
            jnp.einsum("qhd,khd->hqk", queries, key_block, preferred_element_type=jnp.float32)
            * scale
        )
        fresh = jnp.maximum(peak, jnp.max(scores, axis=2))
        expo = jnp.exp(scores - fresh[:, :, None])
        factor = jnp.exp(peak - fresh)
        total = total * factor + jnp.sum(expo, axis=2)
        weighted = jnp.einsum(
            "hqk,khd->qhd",
            expo.astype(jnp.bfloat16),
            value_block,
            preferred_element_type=jnp.float32,
        )
        accum = (accum.reshape(q_rows, heads, width) * factor.T[:, :, None] + weighted).reshape(
            q_rows, heads * width
        )
        return (fresh, total, accum)

    return lax.fori_loop(0, count // size, update, carry)


def start_state(heads, count, features):
    return (
        jnp.full((heads, count), lowest, jnp.float32),
        jnp.zeros((heads, count), jnp.float32),
        jnp.zeros((count, features), jnp.float32),
    )


def per_device(query, key, value, out_weight):
    rows, features = query.shape
    heads = features // HD
    gathered = lax.all_gather(query, "node", axis=0, tiled=True)
    count = gathered.shape[0]
    q_three = gathered.reshape(count, heads, HD)
    peak, total, accum = attend(
        start_state(heads, count, features),
        lax.all_gather(key, "blk", axis=0, tiled=True),
        lax.all_gather(value, "blk", axis=0, tiled=True),
        q_three,
    )
    nodes = lax.axis_size("node")
    acc_parts = accum.reshape(nodes, rows, features)
    peak_parts = peak.T.reshape(nodes, rows, heads)
    total_parts = total.T.reshape(nodes, rows, heads)
    acc_in = lax.all_to_all(acc_parts, "node", split_axis=0, concat_axis=0, tiled=True)
    peak_in = lax.all_to_all(peak_parts, "node", split_axis=0, concat_axis=0, tiled=True)
    total_in = lax.all_to_all(total_parts, "node", split_axis=0, concat_axis=0, tiled=True)
    sources = acc_in.shape[0]
    items = acc_in.shape[1]
    best = jnp.max(peak_in, axis=0)
    weight = jnp.exp(peak_in - best[None])
    summed = jnp.sum(weight * total_in, axis=0)
    joined = jnp.sum(acc_in.reshape(sources, items, heads, HD) * weight[:, :, :, None], axis=0)
    attn = (joined / summed[:, :, None]).reshape(items, features).astype(jnp.bfloat16)
    return lax.psum_scatter(
        jnp.dot(attn, out_weight, preferred_element_type=jnp.float32).astype(jnp.bfloat16),
        "pair",
        scatter_dimension=0,
        tiled=True,
    )


def solution(mesh):
    in_specs = (
        P(("grp", "blk", "node"), "pair"),
        P(("grp", "blk", "node"), "pair"),
        P(("grp", "blk", "node"), "pair"),
        P("pair", None),
    )
    out_specs = P(("grp", "blk", "node", "pair"), None)
    return jax.shard_map(
        per_device, mesh=mesh, in_specs=in_specs, out_specs=out_specs, check_vma=False
    )
```

profile of v0, /device:TPU:0, one launch (start us, length us, event | category | flops | bytes accessed | tf_op | source)
XLA Modules:
  0.0 324.1 jit_solution(2416669906681257392)
XLA Ops:
  6.5 0.0 copy-start
  6.5 0.0 all-gather.6.cloned.1.call-start
  6.5 0.7 all-gather.6.cloned.1.call-update
  7.3 0.0 all-gather.4.cloned.1.call-start
  7.3 0.7 all-gather.4.cloned.1.call-update
  8.0 0.0 all-gather.8.cloned.1.call-start
  8.1 0.7 all-gather.8.cloned.1.call-update
  8.8 22.0 %all-gather.6.cloned.1.call-done = bf16[576,1280]{1,0:T(8,128)(2,1)} async-done(((bf16[144,1280]{1,0:T(8,128)(2,1)}), bf16[576,1280]{1,0:T(8,128)(2,1)}) %all-gather.6.cloned.1.call-update) | async-done | bytes 1474576 | tf_op jit(solution)/shard_map/all_gather | solution.py:65
  30.7 2.7 copy.30
  33.4 57.5 %all-gather.4.cloned.1.call-done = bf16[1152,1280]{1,0:T(8,128)(2,1)} async-done(((bf16[144,1280]{1,0:T(8,128)(2,1)}), bf16[1152,1280]{1,0:T(8,128)(2,1)}) %all-gather.4.cloned.1.call-update) | async-done | bytes 2949136 | tf_op jit(solution)/shard_map/all_gather | solution.py:70
  90.9 58.8 %all-gather.8.cloned.1.call-done = bf16[1152,1280]{1,0:T(8,128)(2,1)} async-done(((bf16[144,1280]{1,0:T(8,128)(2,1)}), bf16[1152,1280]{1,0:T(8,128)(2,1)}) %all-gather.8.cloned.1.call-update) | async-done | bytes 2949136 | tf_op jit(solution)/shard_map/all_gather | solution.py:71
  149.7 1.9 broadcast_in_dim.20
  151.6 106.3 %while.18 = (s32[]{:T(128)}, f32[20,576]{1,0:T(8,128)S(1)}, f32[20,576]{1,0:T(8,128)}, f32[576,1280]{0,1:T(8,128)}, bf16[1152,1280]{1,0:T(8,128)(2,1)}, /*index=...) while((s32[]{:T(128)}, f32[20,576]{1,0:T(8,128)S(1)}, ...), condition=%wide.region_3.0_spmd.clone, body=%wide.region_0.0_spmd.clone.sunk | while | flops 1753320960 | bytes 102850792 | solution.py:51
  151.6 3.7 %constant_dynamic-slice_fusion.3 = (bf16[576,1280]{1,0:T(8,128)(2,1)}, bf16[576,1280]{1,0:T(8,128)(2,1)}) fusion(bf16[1152,1280]{1,0:T(8,128)(2,1)} %get-tuple-element.277, s32[]{:T(128)S(6)} %select_n.10, bf16[1152,1280]{1,0:T(8,128)(2,1)} %get-tuple-element.275), kind=kLoop, calls=%fused_computation.14.clone.1 | loop fusion | bytes 5898244 | tf_op jit(solution)/shard_map/while/body/eval_jaxpr/dynamic_slice | solution.py:29
  155.2 2.7 copy.49
  157.9 15.7 %bitcast_reduce_fusion.3 = (f32[20,576]{1,0:T(8,128)S(1)}, f32[20,576,576]{2,1,0:T(8,128)}) fusion(bf16[576,20,64]{0,2,1:T(8,128)(2,1)} %bitcast.67, bf16[576,20,64]{0,2,1:T(8,128)(2,1)} %get-tuple-element.276), kind=kOutput, calls=%fused_computation.1.clone.1 | convolution fusion | flops 862606080 | bytes 29537280 | tf_op jit(solution)/shard_map/while/body/eval_jaxpr/qhd,khd->hqk/dot_general | solution.py:33
  173.6 0.0 copy-start.1
  173.6 10.4 %fusion.28 = f32[20,576]{1,0:T(8,128)S(1)} fusion(f32[20,576,576]{2,1,0:T(8,128)} %get-tuple-element.246, f32[20,576]{1,0:T(8,128)S(1)} %get-tuple-element.272), kind=kLoop, calls=%fused_computation.4.clone.1 | loop fusion | flops 19895040 | bytes 26634240 | tf_op jit(solution)/shard_map/while/body/eval_jaxpr/reduce_sum | solution.py:39
  184.0 0.0 copy-done.1
  184.0 0.0 copy-start.2
  184.1 2.7 copy.50
  186.7 18.0 %bitcast_add_fusion.2 = f32[576,20,64]{0,2,1:T(8,128)} fusion(f32[576,20,64]{0,2,1:T(8,128)} %bitcast.70, bf16[576,20,64]{0,2,1:T(8,128)(2,1)} %bitcast.69, f32[20,576,576]{2,1,0:T(8,128)} %get-tuple-element.246, f32[20,576]{1,0:T(8,128)S(1)} %get-tuple-element.272, f32[576,20]{0,1:T(8,128)S(1)} %get-tuple-element.248), kind=kOutput, calls=%fused_computation.8.clone.1 | convolution fusion | flops 870727680 | bytes 34007040 | tf_op jit(solution)/shard_map/while/body/eval_jaxpr/hqk,khd->qhd/dot_general | solution.py:40
  204.7 0.0 copy-done.2
  204.7 3.7 %constant_dynamic-slice_fusion.3 = (bf16[576,1280]{1,0:T(8,128)(2,1)}, bf16[576,1280]{1,0:T(8,128)(2,1)}) fusion(bf16[1152,1280]{1,0:T(8,128)(2,1)} %get-tuple-element.277, s32[]{:T(128)S(6)} %select_n.10, bf16[1152,1280]{1,0:T(8,128)(2,1)} %get-tuple-element.275), kind=kLoop, calls=%fused_computation.14.clone.1 | loop fusion | bytes 5898244 | tf_op jit(solution)/shard_map/while/body/eval_jaxpr/dynamic_slice | solution.py:29
  208.4 2.7 copy.49
  211.0 15.7 %bitcast_reduce_fusion.3 = (f32[20,576]{1,0:T(8,128)S(1)}, f32[20,576,576]{2,1,0:T(8,128)}) fusion(bf16[576,20,64]{0,2,1:T(8,128)(2,1)} %bitcast.67, bf16[576,20,64]{0,2,1:T(8,128)(2,1)} %get-tuple-element.276), kind=kOutput, calls=%fused_computation.1.clone.1 | convolution fusion | flops 862606080 | bytes 29537280 | tf_op jit(solution)/shard_map/while/body/eval_jaxpr/qhd,khd->hqk/dot_general | solution.py:33
  226.7 0.0 copy-start.1
  226.7 10.4 %fusion.28 = f32[20,576]{1,0:T(8,128)S(1)} fusion(f32[20,576,576]{2,1,0:T(8,128)} %get-tuple-element.246, f32[20,576]{1,0:T(8,128)S(1)} %get-tuple-element.272), kind=kLoop, calls=%fused_computation.4.clone.1 | loop fusion | flops 19895040 | bytes 26634240 | tf_op jit(solution)/shard_map/while/body/eval_jaxpr/reduce_sum | solution.py:39
  237.1 0.0 copy-done.1
  237.2 0.0 copy-start.2
  237.2 2.7 copy.50
  239.9 18.0 %bitcast_add_fusion.2 = f32[576,20,64]{0,2,1:T(8,128)} fusion(f32[576,20,64]{0,2,1:T(8,128)} %bitcast.70, bf16[576,20,64]{0,2,1:T(8,128)(2,1)} %bitcast.69, f32[20,576,576]{2,1,0:T(8,128)} %get-tuple-element.246, f32[20,576]{1,0:T(8,128)S(1)} %get-tuple-element.272, f32[576,20]{0,1:T(8,128)S(1)} %get-tuple-element.248), kind=kOutput, calls=%fused_computation.8.clone.1 | convolution fusion | flops 870727680 | bytes 34007040 | tf_op jit(solution)/shard_map/while/body/eval_jaxpr/hqk,khd->qhd/dot_general | solution.py:40
  257.9 0.0 copy-done.2
  257.9 0.1 reshape.54
  258.0 0.7 reshape.60
  258.8 3.5 %all-to-all-start.1 = ((f32[4,1,2880]{2,1,0:T(1,128)}), f32[4,1,2880]{2,1,0:T(1,128)S(1)}, u32[]{:S(2)}, u32[]{:S(2)}) async-start(f32[4,1,2880]{2,1,0:T(1,128)} %reshape.60), calls=%async_computation.1 | async-start | bytes 94208 | tf_op jit(solution)/shard_map/all_to_all | solution.py:79
  262.2 0.9 reshape.55
  263.2 0.8 reshape.62
  263.9 2.3 all-to-all-done.1
  266.2 3.3 %all-to-all-start.2 = ((f32[4,1,2880]{2,1,0:T(1,128)}), f32[4,1,2880]{2,1,0:T(1,128)S(1)}, u32[]{:S(2)}, u32[]{:S(2)}) async-start(f32[4,1,2880]{2,1,0:T(1,128)} %reshape.62), calls=%async_computation.2 | async-start | bytes 94208 | tf_op jit(solution)/shard_map/all_to_all | solution.py:80
  269.5 3.6 %copy.33 = f32[576,1280]{1,0:T(8,128)} copy(f32[576,1280]{0,1:T(8,128)} %get-tuple-element.131) | data formatting | bytes 5898240 | tf_op jit(solution)/shard_map/while | solution.py:51
  273.0 0.4 all-to-all-done.2
  273.5 4.6 %all-to-all-start = ((f32[4,144,1280]{2,1,0:T(8,128)}), f32[4,144,1280]{2,1,0:T(8,128)}, u32[]{:S(2)}, u32[]{:S(2)}) async-start(f32[4,144,1280]{2,1,0:T(8,128)} %bitcast.72), calls=%async_computation | async-start | bytes 5898240 | tf_op jit(solution)/shard_map/all_to_all | solution.py:78
  278.1 0.5 broadcast.49
  278.6 0.8 reduce.1
  279.4 0.1 reshape.61
  279.5 0.8 reduce.2
  280.3 0.1 reshape.63
  280.4 0.7 multiply_reduce_fusion.1
  281.1 1.8 copy.35
  282.8 5.3 %mul.59 = f32[4,144,20,64]{3,2,1,0:T(8,128)} broadcast(f32[4,144,20]{2,1,0:T(8,128)} %copy.35), dimensions={0,1,2} | broadcast | bytes 2995200 | tf_op jit(solution)/shard_map/mul | solution.py:86
  288.1 6.4 %mul.60 = f32[4,144,1280]{2,1,0:T(8,128)} reshape(f32[4,144,20,64]{3,2,1,0:T(8,128)} %mul.59) | data formatting | bytes 5898240 | tf_op jit(solution)/shard_map/mul | solution.py:86
  294.5 0.1 copy.38
  294.6 1.8 div.11
  296.4 2.6 div.12
  299.0 14.0 %all-to-all-done = f32[4,144,1280]{2,1,0:T(8,128)} async-done(((f32[4,144,1280]{2,1,0:T(8,128)}), f32[4,144,1280]{2,1,0:T(8,128)}, u32[]{:S(2)}, u32[]{:S(2)}) %all-to-all-start) | async-done | bytes 2949152 | tf_op jit(solution)/shard_map/all_to_all | solution.py:78
  313.0 0.0 copy-start.3
  313.0 3.2 multiply_reduce_fusion
  316.2 0.0 copy-done
  316.2 0.0 copy-done.3
  316.2 1.4 convolution_convert_fusion
  (11 shorter events, 0.2 us)
Async XLA Ops:
  6.5 309.6 %copy-start = (bf16[1280,1280]{1,0:T(8,128)(2,1)S(1)}, bf16[1280,1280]{1,0:T(8,128)(2,1)}, u32[]{:S(2)}) copy-start(bf16[1280,1280]{1,0:T(8,128)(2,1)} %param.9) | copy-start | bytes 9830404
  6.5 24.2 %all-gather.6.cloned.1.call-start = ((), (), s32[]{:S(2)}) async-start(), calls=%async_computation.4 | async-start | bytes 1843200 | tf_op jit(solution)/shard_map/all_gather | solution.py:65
  7.3 83.6 %all-gather.4.cloned.1.call-start = ((), (), s32[]{:S(2)}) async-start(), calls=%async_computation.3 | async-start | bytes 3317760 | tf_op jit(solution)/shard_map/all_gather | solution.py:70
  8.0 141.7 %all-gather.8.cloned.1.call-start = ((), (), s32[]{:S(2)}) async-start(), calls=%async_computation.5 | async-start | bytes 3317760 | tf_op jit(solution)/shard_map/all_gather | solution.py:71
  173.6 10.4 %copy-start.1 = (f32[20,576]{1,0:T(8,128)S(1)}, f32[20,576]{1,0:T(8,128)}, u32[]{:S(2)}) copy-start(f32[20,576]{1,0:T(8,128)} %get-tuple-element.262) | copy-start | bytes 138244 | tf_op jit(solution)/shard_map/while
  184.0 20.7 %copy-start.2 = (f32[20,576]{1,0:T(8,128)}, f32[20,576]{1,0:T(8,128)S(1)}, u32[]{:S(2)}) copy-start(f32[20,576]{1,0:T(8,128)S(1)} %fusion.29) | copy-start | bytes 138244 | tf_op jit(solution)/shard_map/while
  226.7 10.4 %copy-start.1 = (f32[20,576]{1,0:T(8,128)S(1)}, f32[20,576]{1,0:T(8,128)}, u32[]{:S(2)}) copy-start(f32[20,576]{1,0:T(8,128)} %get-tuple-element.262) | copy-start | bytes 138244 | tf_op jit(solution)/shard_map/while
  237.2 20.7 %copy-start.2 = (f32[20,576]{1,0:T(8,128)}, f32[20,576]{1,0:T(8,128)S(1)}, u32[]{:S(2)}) copy-start(f32[20,576]{1,0:T(8,128)S(1)} %fusion.29) | copy-start | bytes 138244 | tf_op jit(solution)/shard_map/while
  258.8 7.4 %all-to-all-start.1 = ((f32[4,1,2880]{2,1,0:T(1,128)}), f32[4,1,2880]{2,1,0:T(1,128)S(1)}, u32[]{:S(2)}, u32[]{:S(2)}) async-start(f32[4,1,2880]{2,1,0:T(1,128)} %reshape.60), calls=%async_computation.1 | async-start | bytes 94208 | tf_op jit(solution)/shard_map/all_to_all | solution.py:79
  266.2 7.3 %all-to-all-start.2 = ((f32[4,1,2880]{2,1,0:T(1,128)}), f32[4,1,2880]{2,1,0:T(1,128)S(1)}, u32[]{:S(2)}, u32[]{:S(2)}) async-start(f32[4,1,2880]{2,1,0:T(1,128)} %reshape.62), calls=%async_computation.2 | async-start | bytes 94208 | tf_op jit(solution)/shard_map/all_to_all | solution.py:80
  273.5 39.5 %all-to-all-start = ((f32[4,144,1280]{2,1,0:T(8,128)}), f32[4,144,1280]{2,1,0:T(8,128)}, u32[]{:S(2)}, u32[]{:S(2)}) async-start(f32[4,144,1280]{2,1,0:T(8,128)} %bitcast.72), calls=%async_computation | async-start | bytes 5898240 | tf_op jit(solution)/shard_map/all_to_all | solution.py:78
  313.0 3.2 copy-start.3
Sparse Core Ops, SparseCore 0:
  8.9 21.7 all-gather.5
  32.9 57.9 all-gather.3
  93.1 56.5 all-gather.7
where the time goes:
time: 325 us; the launch traced here: 324 us
  waiting for transfers between devices  157 us (48%)
  matrix products  68.7 us (21%)
  local copies, waits for them, and re-layouts  47.4 us (15%)
  other arithmetic  26.3 us (8%)
  between operations  13.2 us (4%)
  starting transfers between devices  11.4 us (4%)
    all_gather x1, waiting for transfers between devices, per_device(): lax.all_gather(value, 'blk', axis=0, tiled=True)  58.8 us
    all_gather x1, waiting for transfers between devices, per_device(): lax.all_gather(key, 'blk', axis=0, tiled=True)  57.5 us
    dot_general x2, matrix products, update(): jnp.einsum('hqk,khd->qhd', expo.astype(jnp.bfloat16), value_block, prefer...  36 us
    dot_general x2, matrix products, update(): jnp.einsum('qhd,khd->hqk', queries, key_block, preferred_element_type=jnp...  31.3 us
    all_gather x1, waiting for transfers between devices, per_device(): gathered = lax.all_gather(query, 'node', axis=0, tiled=True)  22 us
    reduce_sum x2, other arithmetic, update(): total = total * factor + jnp.sum(expo, axis=2)  20.8 us
    all_to_all x1, waiting for transfers between devices, per_device(): lax.all_to_all(acc_parts, 'node', split_axis=0, concat_axis=0, tiled=True)  14 us
    dynamic_slice x4, local copies, waits for them, and re-layouts, update(): lax.dynamic_slice_in_dim(values_piece, turn * size, size, 0)  12.7 us
  transfers between devices with their start and end apart: 6, of which 6 were waited for; matrix products, arithmetic and copies ran while one was open for 9% of the time, Pallas kernels for 0%

commit v1 on v0

--- a/solution.py
+++ b/solution.py
@@ -6,6 +6,19 @@
 
 HD = 64
 lowest = -1e30
+
+
+def trace_the_sample(frame_in):
+    named_axis = "node"
+    amount_of = lax.axis_size(named_axis)
+    seen = [(src_i, (src_i + 1) % amount_of) for src_i in range(amount_of)]
+    small = [None] * amount_of
+    small[amount_of - 1] = frame_in
+    for tick in range(amount_of - 2, -1, -1):
+        small[tick] = lax.ppermute(small[tick + 1], axis_name=named_axis, perm=seen)
+    answer = jnp.concatenate(small, axis=0)
+    x_now = (lax.axis_index(named_axis) + 1) * frame_in.shape[0]
+    return jnp.roll(answer, x_now, axis=0)
 
 
 def block_rows(count):
@@ -62,7 +75,7 @@
 def per_device(query, key, value, out_weight):
     rows, features = query.shape
     heads = features // HD
-    gathered = lax.all_gather(query, "node", axis=0, tiled=True)
+    gathered = trace_the_sample(query)
     count = gathered.shape[0]
     q_three = gathered.reshape(count, heads, HD)
     peak, total, accum = attend(

time: 325 us -> 305 us (0.938)
  waiting for transfers between devices: 157 us -> 128 us
  local copies, waits for them, and re-layouts: 47.4 us -> 55.1 us
    all_gather x1, waiting for transfers between devices: 57.5 us -> 29.7 us  [per_device(): lax.all_gather(key, 'blk', axis=0, tiled=True)]
    all_gather x1 -> x0, waiting for transfers between devices: 22 us -> none  [per_device(): gathered = lax.all_gather(query, 'node', axis=0, tiled=True)]
    ppermute x0 -> x3, waiting for transfers between devices: none -> 21.5 us  [trace_the_sample(): small[tick] = lax.ppermute(small[tick + 1], axis_name=named_axis, perm=seen)]
    unnamed x8 -> x21, local copies, waits for them, and re-layouts: 1.72 us -> 7.86 us
    dynamic_slice x0 -> x2, local copies, waits for them, and re-layouts: none -> 4.15 us  [trace_the_sample(): return jnp.roll(answer, x_now, axis=0)]
  transfers between devices with their start and end apart: 6 -> 8, of which waited for: 6 -> 8; matrix products, arithmetic and copies ran while one was open for 9% -> 12% of each run, Pallas kernels for 0% -> 0%
where the time goes in v1:
time: 305 us; the launch traced here: 304 us
  waiting for transfers between devices  128 us (42%)
  matrix products  68.7 us (23%)
  local copies, waits for them, and re-layouts  55.1 us (18%)
  other arithmetic  26.3 us (9%)
  between operations  13.6 us (4%)
  starting transfers between devices  12 us (4%)
    all_gather x1, waiting for transfers between devices, per_device(): lax.all_gather(value, 'blk', axis=0, tiled=True)  58.8 us
    dot_general x2, matrix products, update(): jnp.einsum('hqk,khd->qhd', expo.astype(jnp.bfloat16), value_block, prefer...  36 us
    dot_general x2, matrix products, update(): jnp.einsum('qhd,khd->hqk', queries, key_block, preferred_element_type=jnp...  31.3 us
    all_gather x1, waiting for transfers between devices, per_device(): lax.all_gather(key, 'blk', axis=0, tiled=True)  29.7 us
    ppermute x3, waiting for transfers between devices, trace_the_sample(): small[tick] = lax.ppermute(small[tick + 1], axis_name=named_axis, perm=seen)  21.5 us
    reduce_sum x2, other arithmetic, update(): total = total * factor + jnp.sum(expo, axis=2)  20.8 us
    all_to_all x1, waiting for transfers between devices, per_device(): lax.all_to_all(acc_parts, 'node', split_axis=0, concat_axis=0, tiled=True)  14 us
    dynamic_slice x4, local copies, waits for them, and re-layouts, update(): lax.dynamic_slice_in_dim(values_piece, turn * size, size, 0)  12.7 us
  transfers between devices with their start and end apart: 8, of which 8 were waited for; matrix products, arithmetic and copies ran while one was open for 12% of the time, Pallas kernels for 0%

profile of v1, /device:TPU:0, one launch (start us, length us, event | category | flops | bytes accessed | tf_op | source)
XLA Modules:
  0.0 303.7 jit_solution(9686499163801225804)
XLA Ops:
  6.5 0.0 all-gather.3.cloned.1.call-start
  6.5 0.7 all-gather.3.cloned.1.call-update
  7.3 0.0 all-gather.5.cloned.1.call-start
  7.3 0.7 all-gather.5.cloned.1.call-update
  8.0 0.5 collective-permute-start
  8.6 7.3 %collective-permute-done = bf16[144,1280]{1,0:T(8,128)(2,1)S(1)} collective-permute-done((bf16[144,1280]{1,0:T(8,128)(2,1)}, bf16[144,1280]{1,0:T(8,128)(2,1)S(1)}, u32[]{:S(2)}, u32[]{:S(2)}) %collective-permute-start) | collective-permute-done | bytes 368672 | tf_op jit(solution)/shard_map/ppermute | solution.py:18
  15.9 0.0 collective-permute-start.1
  15.9 7.0 %collective-permute-done.1 = bf16[144,1280]{1,0:T(8,128)(2,1)} collective-permute-done((bf16[144,1280]{1,0:T(8,128)(2,1)S(1)}, bf16[144,1280]{1,0:T(8,128)(2,1)}, u32[]{:S(2)}, u32[]{:S(2)}) %collective-permute-start.1) | collective-permute-done | bytes 368672 | tf_op jit(solution)/shard_map/ppermute | solution.py:18
  22.9 0.0 collective-permute-start.2
  23.0 0.0 copy-start.5
  23.0 0.0 copy-start.3
  23.0 7.2 %collective-permute-done.2 = bf16[144,1280]{1,0:T(8,128)(2,1)} collective-permute-done((bf16[144,1280]{1,0:T(8,128)(2,1)}, bf16[144,1280]{1,0:T(8,128)(2,1)}, u32[]{:S(2)}, u32[]{:S(2)}) %collective-permute-start.2) | collective-permute-done | bytes 368672 | tf_op jit(solution)/shard_map/ppermute | solution.py:18
  30.2 1.0 constant_dynamic-update-slice_fusion.7
  31.2 1.0 constant_dynamic-update-slice_fusion.6
  32.2 1.0 constant_dynamic-update-slice_fusion.5
  33.2 1.0 constant_dynamic-update-slice_fusion.4
  34.3 1.0 constant_dynamic-update-slice_fusion.3
  35.3 1.0 constant_dynamic-update-slice_fusion.2
  36.3 0.0 copy-done.5
  36.4 1.5 constant_dynamic-slice_fusion.2
  37.9 2.7 copy.30
  40.5 29.7 %all-gather.3.cloned.1.call-done = bf16[1152,1280]{1,0:T(8,128)(2,1)} async-done(((bf16[144,1280]{1,0:T(8,128)(2,1)}), bf16[1152,1280]{1,0:T(8,128)(2,1)}) %all-gather.3.cloned.1.call-update) | async-done | bytes 2949136 | tf_op jit(solution)/shard_map/all_gather | solution.py:83
  70.2 58.8 %all-gather.5.cloned.1.call-done = bf16[1152,1280]{1,0:T(8,128)(2,1)} async-done(((bf16[144,1280]{1,0:T(8,128)(2,1)}), bf16[1152,1280]{1,0:T(8,128)(2,1)}) %all-gather.5.cloned.1.call-update) | async-done | bytes 2949136 | tf_op jit(solution)/shard_map/all_gather | solution.py:84
  129.0 1.9 broadcast_in_dim.20
  130.9 106.4 %while.18 = (s32[]{:T(128)}, f32[20,576]{1,0:T(8,128)S(1)}, f32[20,576]{1,0:T(8,128)}, f32[576,1280]{0,1:T(8,128)}, bf16[1152,1280]{1,0:T(8,128)(2,1)}, /*index=...) while((s32[]{:T(128)}, f32[20,576]{1,0:T(8,128)S(1)}, ...), condition=%wide.region_3.4_spmd.clone, body=%wide.region_0.3_spmd.clone.sunk | while | flops 1753320960 | bytes 102850792 | solution.py:64
  130.9 3.7 %constant_dynamic-slice_fusion.4 = (bf16[576,1280]{1,0:T(8,128)(2,1)}, bf16[576,1280]{1,0:T(8,128)(2,1)}) fusion(bf16[1152,1280]{1,0:T(8,128)(2,1)} %get-tuple-element.277, s32[]{:T(128)S(6)} %select_n.25, bf16[1152,1280]{1,0:T(8,128)(2,1)} %get-tuple-element.275), kind=kLoop, calls=%fused_computation.14.clone.1 | loop fusion | bytes 5898244 | tf_op jit(solution)/shard_map/while/body/eval_jaxpr/dynamic_slice | solution.py:42
  134.6 2.7 copy.49
  137.2 15.7 %bitcast_reduce_fusion.3 = (f32[20,576]{1,0:T(8,128)S(1)}, f32[20,576,576]{2,1,0:T(8,128)}) fusion(bf16[576,20,64]{0,2,1:T(8,128)(2,1)} %bitcast.67, bf16[576,20,64]{0,2,1:T(8,128)(2,1)} %get-tuple-element.276), kind=kOutput, calls=%fused_computation.1.clone.1 | convolution fusion | flops 862606080 | bytes 29537280 | tf_op jit(solution)/shard_map/while/body/eval_jaxpr/qhd,khd->hqk/dot_general | solution.py:46
  152.9 10.4 %fusion.28 = f32[20,576]{1,0:T(8,128)S(1)} fusion(f32[20,576,576]{2,1,0:T(8,128)} %get-tuple-element.246, f32[20,576]{1,0:T(8,128)S(1)} %get-tuple-element.272), kind=kLoop, calls=%fused_computation.4.clone.1 | loop fusion | flops 19895040 | bytes 26634240 | tf_op jit(solution)/shard_map/while/body/eval_jaxpr/reduce_sum | solution.py:52
  163.4 0.0 copy-start.2
  163.4 2.7 copy.50
  166.1 18.0 %bitcast_add_fusion.2 = f32[576,20,64]{0,2,1:T(8,128)} fusion(f32[576,20,64]{0,2,1:T(8,128)} %bitcast.70, bf16[576,20,64]{0,2,1:T(8,128)(2,1)} %bitcast.69, f32[20,576,576]{2,1,0:T(8,128)} %get-tuple-element.246, f32[20,576]{1,0:T(8,128)S(1)} %get-tuple-element.272, f32[576,20]{0,1:T(8,128)S(1)} %get-tuple-element.248), kind=kOutput, calls=%fused_computation.8.clone.1 | convolution fusion | flops 870727680 | bytes 34007040 | tf_op jit(solution)/shard_map/while/body/eval_jaxpr/hqk,khd->qhd/dot_general | solution.py:53
  184.1 0.0 copy-done.2
  184.1 3.7 %constant_dynamic-slice_fusion.4 = (bf16[576,1280]{1,0:T(8,128)(2,1)}, bf16[576,1280]{1,0:T(8,128)(2,1)}) fusion(bf16[1152,1280]{1,0:T(8,128)(2,1)} %get-tuple-element.277, s32[]{:T(128)S(6)} %select_n.25, bf16[1152,1280]{1,0:T(8,128)(2,1)} %get-tuple-element.275), kind=kLoop, calls=%fused_computation.14.clone.1 | loop fusion | bytes 5898244 | tf_op jit(solution)/shard_map/while/body/eval_jaxpr/dynamic_slice | solution.py:42
  187.7 2.7 copy.49
  190.4 15.7 %bitcast_reduce_fusion.3 = (f32[20,576]{1,0:T(8,128)S(1)}, f32[20,576,576]{2,1,0:T(8,128)}) fusion(bf16[576,20,64]{0,2,1:T(8,128)(2,1)} %bitcast.67, bf16[576,20,64]{0,2,1:T(8,128)(2,1)} %get-tuple-element.276), kind=kOutput, calls=%fused_computation.1.clone.1 | convolution fusion | flops 862606080 | bytes 29537280 | tf_op jit(solution)/shard_map/while/body/eval_jaxpr/qhd,khd->hqk/dot_general | solution.py:46
  206.1 10.4 %fusion.28 = f32[20,576]{1,0:T(8,128)S(1)} fusion(f32[20,576,576]{2,1,0:T(8,128)} %get-tuple-element.246, f32[20,576]{1,0:T(8,128)S(1)} %get-tuple-element.272), kind=kLoop, calls=%fused_computation.4.clone.1 | loop fusion | flops 19895040 | bytes 26634240 | tf_op jit(solution)/shard_map/while/body/eval_jaxpr/reduce_sum | solution.py:52
  216.6 2.7 copy.50
  219.3 18.0 %bitcast_add_fusion.2 = f32[576,20,64]{0,2,1:T(8,128)} fusion(f32[576,20,64]{0,2,1:T(8,128)} %bitcast.70, bf16[576,20,64]{0,2,1:T(8,128)(2,1)} %bitcast.69, f32[20,576,576]{2,1,0:T(8,128)} %get-tuple-element.246, f32[20,576]{1,0:T(8,128)S(1)} %get-tuple-element.272, f32[576,20]{0,1:T(8,128)S(1)} %get-tuple-element.248), kind=kOutput, calls=%fused_computation.8.clone.1 | convolution fusion | flops 870727680 | bytes 34007040 | tf_op jit(solution)/shard_map/while/body/eval_jaxpr/hqk,khd->qhd/dot_general | solution.py:53
  237.3 0.1 reshape.54
  237.4 0.8 reshape.60
  238.2 3.3 %all-to-all-start.1 = ((f32[4,1,2880]{2,1,0:T(1,128)}), f32[4,1,2880]{2,1,0:T(1,128)S(1)}, u32[]{:S(2)}, u32[]{:S(2)}) async-start(f32[4,1,2880]{2,1,0:T(1,128)} %reshape.60), calls=%async_computation.1 | async-start | bytes 94208 | tf_op jit(solution)/shard_map/all_to_all | solution.py:92
  241.4 0.9 reshape.55
  242.4 0.8 reshape.62
  243.1 2.3 all-to-all-done.1
  245.4 3.5 %all-to-all-start.2 = ((f32[4,1,2880]{2,1,0:T(1,128)}), f32[4,1,2880]{2,1,0:T(1,128)S(1)}, u32[]{:S(2)}, u32[]{:S(2)}) async-start(f32[4,1,2880]{2,1,0:T(1,128)} %reshape.62), calls=%async_computation.2 | async-start | bytes 94208 | tf_op jit(solution)/shard_map/all_to_all | solution.py:93
  248.9 3.6 %copy.33 = f32[576,1280]{1,0:T(8,128)} copy(f32[576,1280]{0,1:T(8,128)} %get-tuple-element.131) | data formatting | bytes 5898240 | tf_op jit(solution)/shard_map/while | solution.py:64
  252.5 0.2 all-to-all-done.2
  252.7 4.6 %all-to-all-start = ((f32[4,144,1280]{2,1,0:T(8,128)}), f32[4,144,1280]{2,1,0:T(8,128)}, u32[]{:S(2)}, u32[]{:S(2)}) async-start(f32[4,144,1280]{2,1,0:T(8,128)} %bitcast.72), calls=%async_computation | async-start | bytes 5898240 | tf_op jit(solution)/shard_map/all_to_all | solution.py:91
  257.3 0.5 broadcast.49
  257.8 0.8 reduce.1
  258.6 0.1 reshape.61
  258.7 0.8 reduce.2
  259.5 0.1 reshape.63
  259.6 0.7 multiply_reduce_fusion.1
  260.3 1.8 copy.35
  262.1 5.3 %mul.63 = f32[4,144,20,64]{3,2,1,0:T(8,128)} broadcast(f32[4,144,20]{2,1,0:T(8,128)} %copy.35), dimensions={0,1,2} | broadcast | bytes 2995200 | tf_op jit(solution)/shard_map/mul | solution.py:99
  267.4 6.4 %mul.64 = f32[4,144,1280]{2,1,0:T(8,128)} reshape(f32[4,144,20,64]{3,2,1,0:T(8,128)} %mul.63) | data formatting | bytes 5898240 | tf_op jit(solution)/shard_map/mul | solution.py:99
  273.7 0.1 copy.38
  273.8 1.8 div.11
  275.6 2.6 div.12
  278.2 14.0 %all-to-all-done = f32[4,144,1280]{2,1,0:T(8,128)} async-done(((f32[4,144,1280]{2,1,0:T(8,128)}), f32[4,144,1280]{2,1,0:T(8,128)}, u32[]{:S(2)}, u32[]{:S(2)}) %all-to-all-start) | async-done | bytes 2949152 | tf_op jit(solution)/shard_map/all_to_all | solution.py:91
  292.2 3.2 %multiply_reduce_fusion = f32[144,1280]{1,0:T(8,128)S(1)} fusion(f32[4,144,1280]{2,1,0:T(8,128)} %all-to-all-done, f32[4,144,1280]{2,1,0:T(8,128)} %mul.64), kind=kLoop, calls=%fused_computation.17 | loop fusion | flops 1290240 | bytes 6635520 | tf_op jit(solution)/shard_map/reduce_sum | solution.py:99
  295.4 1.4 convolution_convert_fusion
  (26 shorter events, 0.3 us)
Async XLA Ops:
  6.5 288.9 %copy-start = (bf16[1280,1280]{1,0:T(8,128)(2,1)S(1)}, bf16[1280,1280]{1,0:T(8,128)(2,1)}, u32[]{:S(2)}) copy-start(bf16[1280,1280]{1,0:T(8,128)(2,1)} %param.9) | copy-start | bytes 9830404
  6.5 63.7 %all-gather.3.cloned.1.call-start = ((), (), s32[]{:S(2)}) async-start(), calls=%async_computation.3 | async-start | bytes 3317760 | tf_op jit(solution)/shard_map/all_gather | solution.py:83
  7.3 121.7 %all-gather.5.cloned.1.call-start = ((), (), s32[]{:S(2)}) async-start(), calls=%async_computation.4 | async-start | bytes 3317760 | tf_op jit(solution)/shard_map/all_gather | solution.py:84
  8.0 7.9 %collective-permute-start = (bf16[144,1280]{1,0:T(8,128)(2,1)}, bf16[144,1280]{1,0:T(8,128)(2,1)S(1)}, u32[]{:S(2)}, u32[]{:S(2)}) collective-permute-start(bf16[144,1280]{1,0:T(8,128)(2,1)} %param.6), channel_id=1, source_target_pairs={{0,1},{1,2},{2,3},{3,0},{4,5},{5,6},{6,7},{7,4},{8,9},{9,10},{10,1... | collective-permute-start | bytes 1105928 | tf_op jit(solution)/shard_map/ppermute | solution.py:18
  15.9 7.0 %copy-start.4 = (bf16[144,1280]{1,0:T(8,128)(2,1)}, bf16[144,1280]{1,0:T(8,128)(2,1)S(1)}, u32[]{:S(2)}) copy-start(bf16[144,1280]{1,0:T(8,128)(2,1)S(1)} %collective-permute-done) | copy-start | bytes 1105924
  15.9 7.0 %collective-permute-start.1 = (bf16[144,1280]{1,0:T(8,128)(2,1)S(1)}, bf16[144,1280]{1,0:T(8,128)(2,1)}, u32[]{:S(2)}, u32[]{:S(2)}) collective-permute-start(bf16[144,1280]{1,0:T(8,128)(2,1)S(1)} %collective-permute-done), channel_id=1, source_target_pairs={{0,1},{1,2},{2,3},{3,0},{4,5},{5,6},{6,7},{7,4},{8,9},{9,10},{10,1... | collective-permute-start | bytes 1105928 | tf_op jit(solution)/shard_map/ppermute | solution.py:18
  22.9 7.3 %collective-permute-start.2 = (bf16[144,1280]{1,0:T(8,128)(2,1)}, bf16[144,1280]{1,0:T(8,128)(2,1)}, u32[]{:S(2)}, u32[]{:S(2)}) collective-permute-start(bf16[144,1280]{1,0:T(8,128)(2,1)} %collective-permute-done.1), channel_id=1, source_target_pairs={{0,1},{1,2},{2,3},{3,0},{4,5},{5,6},{6,7},{7,4},{8,9},{9,10},{10,1... | collective-permute-start | bytes 1105928 | tf_op jit(solution)/shard_map/ppermute | solution.py:18
  23.0 13.3 %copy-start.5 = (bf16[144,1280]{1,0:T(8,128)(2,1)S(1)}, bf16[144,1280]{1,0:T(8,128)(2,1)}, u32[]{:S(2)}) copy-start(bf16[144,1280]{1,0:T(8,128)(2,1)} %copy-done.4) | copy-start | bytes 1105924
  23.0 13.4 %copy-start.3 = (bf16[144,1280]{1,0:T(8,128)(2,1)S(1)}, bf16[144,1280]{1,0:T(8,128)(2,1)}, u32[]{:S(2)}) copy-start(bf16[144,1280]{1,0:T(8,128)(2,1)} %param.6) | copy-start | bytes 1105924
  152.9 10.4 %copy-start.1 = (f32[20,576]{1,0:T(8,128)S(1)}, f32[20,576]{1,0:T(8,128)}, u32[]{:S(2)}) copy-start(f32[20,576]{1,0:T(8,128)} %get-tuple-element.262) | copy-start | bytes 138244 | tf_op jit(solution)/shard_map/while
  163.4 20.7 %copy-start.2 = (f32[20,576]{1,0:T(8,128)}, f32[20,576]{1,0:T(8,128)S(1)}, u32[]{:S(2)}) copy-start(f32[20,576]{1,0:T(8,128)S(1)} %fusion.29) | copy-start | bytes 138244 | tf_op jit(solution)/shard_map/while
  206.1 10.4 %copy-start.1 = (f32[20,576]{1,0:T(8,128)S(1)}, f32[20,576]{1,0:T(8,128)}, u32[]{:S(2)}) copy-start(f32[20,576]{1,0:T(8,128)} %get-tuple-element.262) | copy-start | bytes 138244 | tf_op jit(solution)/shard_map/while
  216.6 20.7 %copy-start.2 = (f32[20,576]{1,0:T(8,128)}, f32[20,576]{1,0:T(8,128)S(1)}, u32[]{:S(2)}) copy-start(f32[20,576]{1,0:T(8,128)S(1)} %fusion.29) | copy-start | bytes 138244 | tf_op jit(solution)/shard_map/while
  238.2 7.3 %all-to-all-start.1 = ((f32[4,1,2880]{2,1,0:T(1,128)}), f32[4,1,2880]{2,1,0:T(1,128)S(1)}, u32[]{:S(2)}, u32[]{:S(2)}) async-start(f32[4,1,2880]{2,1,0:T(1,128)} %reshape.60), calls=%async_computation.1 | async-start | bytes 94208 | tf_op jit(solution)/shard_map/all_to_all | solution.py:92
  245.4 7.3 %all-to-all-start.2 = ((f32[4,1,2880]{2,1,0:T(1,128)}), f32[4,1,2880]{2,1,0:T(1,128)S(1)}, u32[]{:S(2)}, u32[]{:S(2)}) async-start(f32[4,1,2880]{2,1,0:T(1,128)} %reshape.62), calls=%async_computation.2 | async-start | bytes 94208 | tf_op jit(solution)/shard_map/all_to_all | solution.py:93
  252.7 39.5 %all-to-all-start = ((f32[4,144,1280]{2,1,0:T(8,128)}), f32[4,144,1280]{2,1,0:T(8,128)}, u32[]{:S(2)}, u32[]{:S(2)}) async-start(f32[4,144,1280]{2,1,0:T(8,128)} %bitcast.72), calls=%async_computation | async-start | bytes 5898240 | tf_op jit(solution)/shard_map/all_to_all | solution.py:91
  292.2 3.2 %copy-start.6 = (f32[144,1280]{1,0:T(8,128)S(1)}, f32[144,1280]{1,0:T(8,128)}, u32[]{:S(2)}) copy-start(f32[144,1280]{1,0:T(8,128)} %div.12) | copy-start | bytes 2211844
Sparse Core Ops, SparseCore 0:
  9.5 60.6 all-gather.2
  72.4 56.5 all-gather.4
